TPU v7x, 32 devices: a whole 2x2x4 slice. The times are simulated.
32 devices in a mesh: dom: 8 (over y, x, core), col: 4 (over z).
Axes of the slice: x: 2, y: 2, z: 4, core: 2. Of those that a mesh axis runs over, the one named last changes fastest.
Arguments:
- features: bfloat16 [65536, 1024], P('dom', 'col')
- weight: bfloat16 [1024, 1024], P(None, 'col'), may hold values from -0.1875 to 0.1875
- out_bias: bfloat16 [1024], P('col'), may hold values from -3 to 3
- local_index: int32 [8, 64, 4], P('dom'), may hold values from 0 to 63
- local_count: int32 [8, 64], P('dom'), may hold values from 1 to 4, as said below
- local_vals: bfloat16 [8, 64, 4, 128, 128], P('dom'), may hold values from -0.1875 to 0.1875
- halo_index: int32 [8, 64, 4], P('dom'), may hold values from 0 to 31
- halo_count: int32 [8, 64], P('dom'), may hold values from 0 to 4, as said below
- halo_vals: bfloat16 [8, 64, 4, 128, 128], P('dom'), may hold values from -0.1875 to 0.1875
- send_rows: int32 [8, 8, 512], P('dom'), may hold values from 0 to 8191
- send_count: int32 [8, 8], P('dom'), may hold values from 0 to 512, as said below
Outputs:
- normalized: bfloat16 [65536, 1024], P('dom', 'col')
- channel_stats: float32 [2, 1024], P(None, 'col')
Inputs may be any that keep to these rules, and one draw needn't show every extreme that they name: `local_index`: slots k >= local_count of a row tile are not used. `local_count`: every partition has a row tile with all 4 slots used. `halo_index`: slots k >= halo_count of a row tile are not used. `halo_count`: every partition has a row tile with all 4 slots used. `send_rows`: slots s >= send_count[q, p] are not used. send_count[p, p] is 0; every partition fills all 512 slots to some other partition.
All inputs are finite; a program needn't handle non-finite values.
Results may differ from a plain program's by a relative error of at most 0.0075.
Values may be sent and summed in bfloat16 or wider, within the bound.
A program may use at most 192 MiB of HBM per device.

v0:
```python
import functools

import jax
import jax.numpy as jnp
from jax import lax
from jax.experimental import pallas as pl
from jax.experimental.pallas import tpu as pltpu
from jax.sharding import PartitionSpec as P

TILE = 128
MESH = pl.DeviceIdType.MESH
CHUNK_TILES = 2
epsilon = 1e-06


def remote(src, dst, send_sem, recv_sem, device):
    return pltpu.make_async_remote_copy(
        src_ref=src,
        dst_ref=dst,
        send_sem=send_sem,
        recv_sem=recv_sem,
        device_id=device,
        device_id_type=MESH,
    )


def kernel(
    n_dom,
    n_col,
    node_total,
    feat_hbm,
    weight_ref,
    bias_ref,
    lidx,
    lcnt,
    lvals_hbm,
    hidx,
    hcnt,
    hvals_hbm,
    srows,
    scnt,
    out_hbm,
    stat_ref,
    xb,
    xf,
    stage,
    outgoing,
    halo,
    lvals,
    hvals,
    wfull,
    bfull,
    tx,
    rx,
    tx2,
    acc,
    part,
    part_in,
    colpart,
    colpart_in,
    in_sem,
    halo_s,
    halo_r,
    w_s,
    w_r,
    wp_s,
    wp_r,
    b_s,
    b_r,
    p1_s,
    p1_r,
    p2_s,
    p2_r,
    own_sem,
    sd_s,
    sd_r,
    sc_s,
    sc_r,
):
    d = lax.axis_index("dom")
    z = lax.axis_index("col")
    rows, width = xf.shape
    slot_total = srows.shape[1]
    k_local = lvals.shape[1]
    k_halo = hvals.shape[1]
    f_total = weight_ref.shape[0]
    tiles_q = rows // TILE // n_col
    rows_q = tiles_q * TILE
    ct = CHUNK_TILES
    r_chunk = ct * TILE
    steps = tiles_q // ct
    per_peer = slot_total // TILE
    half = f_total // 2

    pieces = in_sem.shape[0] - 2
    piece = rows // TILE // pieces

    def feat_copy(i):
        at = pl.ds(i * piece, piece)
        return pltpu.make_async_copy(feat_hbm.at[at], xb.at[at], in_sem.at[2 + i])

    for i in range(pieces):
        feat_copy(i).start()
    bfull[z] = jnp.broadcast_to(bias_ref[...], bfull.shape[1:])

    barrier = pltpu.get_barrier_semaphore()
    for o in range(1, n_dom):
        pl.semaphore_signal(barrier, inc=1, device_id=(lax.rem(d + o, n_dom), z), device_id_type=MESH)
    for o in range(1, n_col):
        pl.semaphore_signal(barrier, inc=1, device_id=(d, lax.rem(z + o, n_col)), device_id_type=MESH)
    pl.semaphore_wait(barrier, n_dom - 1 + n_col - 1)

    core = lax.rem(d, 2)
    mate = d + 1 - 2 * core
    my_half = pl.ds(pl.multiple_of(core * half, half), half)

    def w_copy(o):
        return remote(
            weight_ref.at[my_half],
            wfull.at[z, my_half],
            w_s.at[o - 1],
            w_r.at[o - 1],
            (d, lax.rem(z + o, n_col)),
        )

    def w_pass(o):
        src = lax.rem(z + n_col - o, n_col)
        return remote(
            wfull.at[src, my_half], wfull.at[src, my_half], wp_s.at[o - 1], wp_r.at[o - 1], (mate, z)
        )

    def b_copy(o):
        return remote(
            bfull.at[z], bfull.at[z], b_s.at[o - 1], b_r.at[o - 1], (d, lax.rem(z + o, n_col))
        )

    for o in range(1, n_col):
        w_copy(o).start()

    lv_copy = pltpu.make_async_copy(lvals_hbm, lvals, in_sem.at[0])
    hv_copy = pltpu.make_async_copy(hvals_hbm, hvals, in_sem.at[1])
    lv_copy.start()
    hv_copy.start()

    @pl.loop(0, pieces)
    def _(i):
        feat_copy(i).wait()
        for j in range(piece):
            t = i * piece + j
            at = pl.ds(pl.multiple_of(t * TILE, TILE), TILE)
            xf[at, :] = xb[t].astype(jnp.float32)

    def peer_of(o):
        return lax.rem(d + (1 - 2 * core) * o + n_dom, n_dom)

    def halo_copy(o):
        return remote(
            outgoing.at[o],
            halo.at[pl.ds(d * per_peer, per_peer)],
            halo_s.at[o],
            halo_r.at[o],
            (peer_of(o), z),
        )

    @pl.loop(0, n_dom - 1)
    def _(i):
        o = lax.rem(i + 1, n_dom - 1) + 1
        peer = peer_of(o)

        @pl.loop(0, slot_total // 16)
        def _(g):
            for k in range(16):
                at = g * 16 + k
                stage[at] = xf[srows[peer, at]]

        used = lax.broadcasted_iota(jnp.int32, (slot_total, width), 0) < scnt[0, peer]
        sent = jnp.where(used, stage[...], 0.0).astype(outgoing.dtype)
        outgoing[o] = sent.reshape(slot_total // TILE, TILE, width)
        halo_copy(o).start()

    halo[pl.ds(d * per_peer, per_peer)] = jnp.zeros((per_peer, TILE, width), halo.dtype)
    wfull[z] = weight_ref[...]

    for o in range(1, n_col):
        w_copy(o).wait_recv()
        w_pass(o).start()
        b_copy(o).start()

    lv_copy.wait()
    hv_copy.wait()

    @pl.loop(1, n_dom)
    def _(o):
        halo_copy(o).wait()

    def kept(count, k):
        one = jnp.minimum(jnp.maximum(count - k, 0), 1).astype(jnp.float32)
        return jnp.broadcast_to(one, (TILE, TILE)).astype(jnp.bfloat16)

    def tile_rows(t):
        lhs, rhs = [], []
        n_loc, n_hal = lcnt[0, t], hcnt[0, t]
        for k in range(k_local):
            v = lvals[t, k]
            lhs.append(v * kept(n_loc, k))
            rhs.append(xb[lidx[k, t]])
        for k in range(k_halo):
            v = hvals[t, k]
            lhs.append(v * kept(n_hal, k))
            rhs.append(halo[hidx[k, t]])
        total = jnp.dot(
            jnp.concatenate(lhs, axis=1),
            jnp.concatenate(rhs, axis=0),
            preferred_element_type=jnp.float32,
        )
        return total.astype(jnp.bfloat16)

    my_cols = pl.ds(pl.multiple_of(z * width, width), width)

    def p1_copy(s, o):
        return remote(
            tx.at[s, o - 1],
            rx.at[s, :, my_cols],
            p1_s.at[s, o - 1],
            p1_r.at[s, o - 1],
            (d, lax.rem(z + o, n_col)),
        )

    @pl.loop(0, steps)
    def _(s):
        for o in range(1, n_col):
            q = lax.rem(z + o, n_col)
            for c in range(ct):
                tx[s, o - 1, c * TILE : (c + 1) * TILE, :] = tile_rows(q * tiles_q + s * ct + c)
            p1_copy(s, o).start()
        for c in range(ct):
            rx[s, c * TILE : (c + 1) * TILE, my_cols] = tile_rows(z * tiles_q + s * ct + c)

    for o in range(1, n_col):
        w_pass(o).wait()
        b_copy(o).wait()
        w_copy(o).wait_send()

    acc[...] = jnp.zeros_like(acc)

    def out_rows(s):
        return pl.ds(pl.multiple_of(z * rows_q + s * r_chunk, r_chunk), r_chunk)

    def p2_copy(s, o):
        q = lax.rem(z + o, n_col)
        return remote(
            tx2.at[s, q],
            out_hbm.at[out_rows(s)],
            p2_s.at[s, o - 1],
            p2_r.at[s, o - 1],
            (d, q),
        )

    def own_copy(s):
        return pltpu.make_async_copy(tx2.at[s, z], out_hbm.at[out_rows(s)], own_sem.at[s])

    @pl.loop(0, steps)
    def _(s):
        for o in range(1, n_col):
            p1_copy(s, o).wait_recv()
        power = jnp.zeros((r_chunk, 1), jnp.float32)
        active = []
        for j in range(n_col):
            y = jnp.dot(rx[s], wfull[j], preferred_element_type=jnp.float32)
            y = jnp.maximum(y + bfull[j][0:1, :].astype(jnp.float32), 0.0)
            power = power + jnp.sum(y * y, axis=1, keepdims=True)
            active.append(y)
        factor = lax.rsqrt(power / f_total + epsilon)
        for j in range(n_col):
            scaled = active[j] * factor
            tx2[s, j] = scaled.astype(jnp.bfloat16)
            grouped = scaled.reshape(r_chunk // 8, 8, width)
            acc[j, 0] += jnp.sum(grouped, axis=0)
            acc[j, 1] += jnp.sum(grouped * grouped, axis=0)
        for o in range(1, n_col):
            p2_copy(s, o).start()
        own_copy(s).start()

    for j in range(n_col):
        part[j] = jnp.concatenate(
            [
                jnp.sum(acc[j, 0], axis=0, keepdims=True),
                jnp.sum(acc[j, 1], axis=0, keepdims=True),
                jnp.zeros((6, width), jnp.float32),
            ],
            axis=0,
        )

    def sd_copy(o):
        return remote(part, part_in.at[o], sd_s.at[o], sd_r.at[o], (lax.rem(d + o, n_dom), z))

    @pl.loop(1, n_dom)
    def _(o):
        sd_copy(o).start()

    part_in[0] = part[...]

    @pl.loop(1, n_dom)
    def _(o):
        sd_copy(o).wait()

    colpart[...] = jnp.sum(part_in[...], axis=0)

    def sc_copy(o):
        q = lax.rem(z + o, n_col)
        return remote(colpart.at[q], colpart_in.at[o], sc_s.at[o - 1], sc_r.at[o - 1], (d, q))

    for o in range(1, n_col):
        sc_copy(o).start()
    colpart_in[0] = colpart[z]

    @pl.loop(0, steps)
    def _(s):
        for o in range(1, n_col):
            p1_copy(s, o).wait_send()
            p2_copy(s, o).wait()
        own_copy(s).wait()

    for o in range(1, n_col):
        sc_copy(o).wait()
    totals = jnp.sum(colpart_in[...], axis=0) / node_total
    mean = totals[0:1, :]
    stat_ref[...] = jnp.concatenate([mean, totals[1:2, :] - mean * mean], axis=0)


def on_device(
    features,
    weight,
    out_bias,
    local_index,
    local_count,
    local_vals,
    halo_index,
    halo_count,
    halo_vals,
    send_rows,
    send_count,
):
    rows, width = features.shape
    n_dom = lax.axis_size("dom")
    n_col = lax.axis_size("col")
    slot_total = send_rows.shape[2]
    f_total = weight.shape[0]
    steps = rows // TILE // n_col // CHUNK_TILES
    r_chunk = CHUNK_TILES * TILE
    any_spec = pl.BlockSpec(memory_space=pl.ANY)
    vmem = pl.BlockSpec(memory_space=pltpu.VMEM)
    smem = pl.BlockSpec(memory_space=pltpu.SMEM)
    bf16, f32 = jnp.bfloat16, jnp.float32
    dma = pltpu.SemaphoreType.DMA
    halo_bytes = 4 * n_dom * slot_total * width
    grant = 44 * 2**20 + 2 * halo_bytes
    held = pltpu.VMEM if grant + 2 * rows * width < 58 * 2**20 else jax.ShapeDtypeStruct
    grant = grant if held is pltpu.VMEM else 67043328
    normalized, stats = pl.pallas_call(
        functools.partial(kernel, n_dom, n_col, rows * n_dom),
        out_shape=(
            held((rows, width), bf16),
            jax.ShapeDtypeStruct((2, width), f32),
        ),
        in_specs=[any_spec, vmem, vmem, smem, smem, any_spec, smem, smem, any_spec, smem, smem],
        out_specs=(any_spec, vmem),
        scratch_shapes=[
            pltpu.VMEM((rows // TILE, TILE, width), bf16),
            pltpu.VMEM((rows, width), f32),
            pltpu.VMEM((slot_total, width), f32),
            pltpu.VMEM((n_dom, slot_total // TILE, TILE, width), bf16),
            pltpu.VMEM((n_dom * slot_total // TILE, TILE, width), bf16),
            pltpu.VMEM(local_vals.shape[1:], bf16),
            pltpu.VMEM(halo_vals.shape[1:], bf16),
            pltpu.VMEM((n_col, f_total, width), bf16),
            pltpu.VMEM((n_col, 16, width), bf16),
            pltpu.VMEM((steps, n_col - 1, r_chunk, width), bf16),
            pltpu.VMEM((steps, r_chunk, n_col * width), bf16),
            pltpu.VMEM((steps, n_col, r_chunk, width), bf16),
            pltpu.VMEM((n_col, 2, 8, width), f32),
            pltpu.VMEM((n_col, 8, width), f32),
            pltpu.VMEM((n_dom, n_col, 8, width), f32),
            pltpu.VMEM((n_col, 8, width), f32),
            pltpu.VMEM((n_col, 8, width), f32),
            dma((10 if rows // TILE % 8 == 0 else 3,)),
            dma((n_dom,)),
            dma((n_dom,)),
            dma((n_col - 1,)),
            dma((n_col - 1,)),
            dma((n_col - 1,)),
            dma((n_col - 1,)),
            dma((n_col - 1,)),
            dma((n_col - 1,)),
            dma((steps, n_col - 1)),
            dma((steps, n_col - 1)),
            dma((steps, n_col - 1)),
            dma((steps, n_col - 1)),
            dma((steps,)),
            dma((n_dom,)),
            dma((n_dom,)),
            dma((n_col - 1,)),
            dma((n_col - 1,)),
        ],
        compiler_params=pltpu.CompilerParams(
            collective_id=0, has_side_effects=True, vmem_limit_bytes=grant
        ),
    )(
        features.reshape(rows // TILE, TILE, width),
        weight,
        out_bias.reshape(1, width),
        local_index[0].T,
        local_count,
        local_vals[0],
        halo_index[0].T,
        halo_count,
        halo_vals[0],
        send_rows[0],
        send_count,
    )
    return normalized, stats


def solution(mesh):
    in_specs = (
        P("dom", "col"),
        P(None, "col"),
        P("col"),
        P("dom", None, None),
        P("dom", None),
        P("dom", None, None, None, None),
        P("dom", None, None),
        P("dom", None),
        P("dom", None, None, None, None),
        P("dom", None, None),
        P("dom", None),
    )
    out_specs = (P("dom", "col"), P(None, "col"))
    return jax.shard_map(
        on_device, mesh=mesh, in_specs=in_specs, out_specs=out_specs, check_vma=False
    )
```

profile of v0, /device:TPU:1, one launch (start us, length us, event | category | flops | bytes accessed | tf_op | source)
XLA Modules:
  0.0 225.4 jit_solution(13610093944138380636)
XLA Ops:
  0.6 1.2 reshape.11.bias_ref
  1.9 221.0 %shard_map.122 = (bf16[8192,256]{1,0:T(8,128)(2,1)S(1)}, f32[2,256]{1,0:T(2,128)}) custom-call(bf16[64,128,256]{2,1,0:T(8,128)(2,1)} %bitcast.12, bf16[1024,256]{1,0:T(8,128)(2,1)} %weight_ref.1, bf16[1,256]{1,0:T(2,128)(2,1)} %reshape.11.bias_ref, s32[4,64]{1,0:T(4,128)} %bitcast.14, s32[1,64]{1,0:T(1,128)} %lcnt.1, bf16[64,4,128,128]{3,2,1,0:T(8,128)(2,1)} %bitcast.10, ...), custom_call_target="tpu_custom_call" | custom-call | tf_op jit(solution)/shard_map/pallas_call | solution.py:360
  222.8 0.0 copy-start
  222.8 2.0 copy.15
  224.8 0.0 copy-done
  224.8 0.6 copy.16
Async XLA Ops:
  222.8 2.0 copy-start
where the time goes:
time: 227 us; the launch traced here: 225 us
  Pallas kernels  221 us (97%)
  local copies, waits for them, and re-layouts  3.82 us (2%)
    pallas_call x1, Pallas kernels, on_device(): pl.pallas_call(functools.partial(kernel, n_dom, n_col, rows * n_dom), out...  221 us

commit v1 on v0

v1 whole, which is shorter than its diff:
```python
import functools

import jax
import jax.numpy as jnp
from jax import lax
from jax.experimental import pallas as pl
from jax.experimental.pallas import tpu as pltpu
from jax.sharding import PartitionSpec as P

TILE = 128
MESH = pl.DeviceIdType.MESH
LANES = 128
P1_TILES = 4
P2_TILES = 2
epsilon = 1e-06


def remote(src, dst, send_sem, recv_sem, device):
    return pltpu.make_async_remote_copy(
        src_ref=src,
        dst_ref=dst,
        send_sem=send_sem,
        recv_sem=recv_sem,
        device_id=device,
        device_id_type=MESH,
    )


def kernel(
    n_dom,
    n_col,
    node_total,
    feat_hbm,
    weight_hbm,
    bias_ref,
    lidx,
    lcnt,
    lvals_hbm,
    hidx,
    hcnt,
    hvals_hbm,
    srows,
    scnt,
    out_hbm,
    stat_ref,
    xb,
    xf,
    stage,
    outgoing,
    halo_a,
    halo_b,
    lvals,
    hvals,
    wfull,
    bfull,
    tx,
    rx,
    tx2,
    acc,
    part,
    part_in,
    colpart,
    colpart_in,
    feat_sem,
    vals_sem,
    wl_sem,
    halo_s,
    halo_r,
    w_s,
    w_r,
    wp_s,
    wp_r,
    b_s,
    b_r,
    p1_s,
    p1_r,
    p2_s,
    p2_r,
    own_sem,
    sd_s,
    sd_r,
    sc_s,
    sc_r,
):
    d = lax.axis_index("dom")
    z = lax.axis_index("col")
    halos = (halo_a, halo_b)
    n_part, rows, lanes = xf.shape
    width = n_part * lanes
    slot_total = srows.shape[1]
    k_local = lvals.shape[1]
    k_halo = hvals.shape[1]
    f_total = weight_hbm.shape[0]
    tiles_q = rows // TILE // n_col
    rows_q = tiles_q * TILE
    ct = P1_TILES
    r_chunk = ct * TILE
    steps = tiles_q // ct
    r_out = P2_TILES * TILE
    halves = r_chunk // r_out
    per_peer = slot_total // TILE
    shard = f_total // n_dom
    n_chips = n_dom // 2
    chip = d // 2
    core = lax.rem(d, 2)
    mate = d + 1 - 2 * core

    pieces = feat_sem.shape[1]
    piece = rows // TILE // pieces

    def feat_copy(c, i):
        at = pl.ds(i * piece, piece)
        return pltpu.make_async_copy(
            feat_hbm.at[at, :, pl.ds(c * lanes, lanes)], xb.at[c, at], feat_sem.at[c, i]
        )

    def w_load():
        mine = pl.ds(pl.multiple_of(d * shard, shard), shard)
        return pltpu.make_async_copy(weight_hbm.at[mine], wfull.at[z, d], wl_sem)

    for i in range(pieces):
        feat_copy(0, i).start()
    w_load().start()
    for i in range(pieces):
        feat_copy(1, i).start()
    bfull[z] = jnp.broadcast_to(bias_ref[...], bfull.shape[1:])

    barrier = pltpu.get_barrier_semaphore()
    for o in range(1, n_dom):
        pl.semaphore_signal(barrier, inc=1, device_id=(lax.rem(d + o, n_dom), z), device_id_type=MESH)
    for o in range(1, n_col):
        pl.semaphore_signal(barrier, inc=1, device_id=(d, lax.rem(z + o, n_col)), device_id_type=MESH)
    pl.semaphore_wait(barrier, n_dom - 1 + n_col - 1)

    def w_copy(o):
        return remote(
            wfull.at[z, d], wfull.at[z, d], w_s.at[o - 1], w_r.at[o - 1], (d, lax.rem(z + o, n_col))
        )

    def w_arrived(o):
        src = lax.rem(z + n_col - o, n_col)
        return remote(
            wfull.at[src, d], wfull.at[src, d], w_s.at[o - 1], w_r.at[o - 1], (d, src)
        )

    def w_pass(o):
        return remote(
            wfull.at[:, d], wfull.at[:, d], wp_s.at[o], wp_r.at[o], (lax.rem(d + o, n_dom), z)
        )

    def w_passed(o):
        src = lax.rem(d + n_dom - o, n_dom)
        return remote(wfull.at[:, src], wfull.at[:, src], wp_s.at[o], wp_r.at[o], (src, z))

    def b_copy(o):
        return remote(
            bfull.at[z], bfull.at[z], b_s.at[o - 1], b_r.at[o - 1], (d, lax.rem(z + o, n_col))
        )

    w_load().wait()
    for o in range(1, n_col):
        w_copy(o).start()
        b_copy(o).start()

    def widen(c):
        @pl.loop(0, pieces)
        def _(i):
            feat_copy(c, i).wait()
            for j in range(piece):
                t = i * piece + j
                xf[c, pl.ds(pl.multiple_of(t * TILE, TILE), TILE), :] = xb[c, t].astype(jnp.float32)

    def slots_of(q):
        return pl.ds(q * per_peer, per_peer)

    def halo_send(c, peer):
        return remote(
            outgoing.at[c, peer],
            halos[c].at[slots_of(d)],
            halo_s.at[c, peer],
            halo_r.at[c, d],
            (peer, z),
        )

    def halo_arrived(c, src):
        return remote(
            outgoing.at[c, src],
            halos[c].at[slots_of(src)],
            halo_s.at[c, src],
            halo_r.at[c, src],
            (src, z),
        )

    def gather(c, peer):
        @pl.loop(0, slot_total // 16)
        def _(g):
            for k in range(16):
                at = g * 16 + k
                stage[at] = xf[c, srows[peer, at]]

        used = lax.broadcasted_iota(jnp.int32, (slot_total, lanes), 0) < scnt[0, peer]
        sent = jnp.where(used, stage[...], 0.0).astype(outgoing.dtype)
        outgoing[c, peer] = sent.reshape(per_peer, TILE, lanes)
        halo_send(c, peer).start()

    def gather_all(c):
        @pl.loop(1, n_chips)
        def _(j):
            gather(c, 2 * lax.rem(chip + j, n_chips))

        gather(c, mate)

        @pl.loop(1, n_chips)
        def _(j):
            gather(c, 2 * lax.rem(chip + j, n_chips) + 1)

    lv_copy = pltpu.make_async_copy(lvals_hbm, lvals, vals_sem.at[0])
    hv_copy = pltpu.make_async_copy(hvals_hbm, hvals, vals_sem.at[1])

    widen(0)
    lv_copy.start()
    hv_copy.start()
    gather_all(0)
    widen(1)
    gather_all(1)
    for c in range(n_part):
        halos[c][slots_of(d)] = jnp.zeros((per_peer, TILE, lanes), halo_a.dtype)

    lv_copy.wait()
    hv_copy.wait()

    def kept(count, k):
        one = jnp.minimum(jnp.maximum(count - k, 0), 1).astype(jnp.float32)
        return jnp.broadcast_to(one, (TILE, TILE)).astype(jnp.bfloat16)

    def tile_rows(c, t):
        lhs, rhs = [], []
        n_loc, n_hal = lcnt[0, t], hcnt[0, t]
        for k in range(k_local):
            lhs.append(lvals[t, k] * kept(n_loc, k))
            rhs.append(xb[c, lidx[k, t]])
        for k in range(k_halo):
            lhs.append(hvals[t, k] * kept(n_hal, k))
            rhs.append(halos[c][hidx[k, t]])
        total = jnp.dot(
            jnp.concatenate(lhs, axis=1),
            jnp.concatenate(rhs, axis=0),
            preferred_element_type=jnp.float32,
        )
        return total.astype(jnp.bfloat16)

    def my_cols(c):
        return pl.ds(pl.multiple_of(z * width + c * lanes, lanes), lanes)

    def p1_copy(c, s, o):
        return remote(
            tx.at[c, s, o - 1],
            rx.at[s, :, my_cols(c)],
            p1_s.at[c, s, o - 1],
            p1_r.at[c, s, o - 1],
            (d, lax.rem(z + o, n_col)),
        )

    for c in range(n_part):

        @pl.loop(1, n_dom)
        def _(o):
            halo_arrived(c, lax.rem(d + o, n_dom)).wait_recv()

        @pl.loop(0, steps)
        def _(s):
            for o in range(1, n_col):
                q = lax.rem(z + o, n_col)
                for i in range(ct):
                    tx[c, s, o - 1, i * TILE : (i + 1) * TILE, :] = tile_rows(c, q * tiles_q + s * ct + i)
                p1_copy(c, s, o).start()
            for i in range(ct):
                rx[s, i * TILE : (i + 1) * TILE, my_cols(c)] = tile_rows(c, z * tiles_q + s * ct + i)

        if c == 0:
            for o in range(1, n_col):
                w_arrived(o).wait_recv()

            @pl.loop(1, n_dom)
            def _(o):
                w_pass(o).start()

    @pl.loop(1, n_dom)
    def _(o):
        w_passed(o).wait_recv()

    for o in range(1, n_col):
        b_copy(o).wait()

    acc[...] = jnp.zeros_like(acc)

    def out_rows(s):
        return pl.ds(pl.multiple_of(z * rows_q + s * r_out, r_out), r_out)

    def p2_copy(s, o):
        q = lax.rem(z + o, n_col)
        return remote(
            tx2.at[s, q],
            out_hbm.at[out_rows(s)],
            p2_s.at[s, o - 1],
            p2_r.at[s, o - 1],
            (d, q),
        )

    def own_copy(s):
        return pltpu.make_async_copy(tx2.at[s, z], out_hbm.at[out_rows(s)], own_sem.at[s])

    @pl.loop(0, steps)
    def _(s):
        for c in range(n_part):
            for o in range(1, n_col):
                p1_copy(c, s, o).wait_recv()

        @pl.loop(0, halves)
        def _(h):
            k = s * halves + h
            mixed = rx[s, pl.ds(pl.multiple_of(h * r_out, r_out), r_out), :]
            power = jnp.zeros((r_out, 1), jnp.float32)
            active = []
            for j in range(n_col):
                y = jnp.dot(
                    mixed, wfull[j].reshape(f_total, width), preferred_element_type=jnp.float32
                )
                y = jnp.maximum(y + bfull[j][0:1, :].astype(jnp.float32), 0.0)
                power = power + jnp.sum(y * y, axis=1, keepdims=True)
                active.append(y)
            factor = lax.rsqrt(power / f_total + epsilon)
            for j in range(n_col):
                scaled = active[j] * factor
                tx2[k, j] = scaled.astype(jnp.bfloat16)
                grouped = scaled.reshape(r_out // 8, 8, width)
                acc[j, 0] += jnp.sum(grouped, axis=0)
                acc[j, 1] += jnp.sum(grouped * grouped, axis=0)
            for o in range(1, n_col):
                p2_copy(k, o).start()
            own_copy(k).start()

    for j in range(n_col):
        part[j] = jnp.concatenate(
            [
                jnp.sum(acc[j, 0], axis=0, keepdims=True),
                jnp.sum(acc[j, 1], axis=0, keepdims=True),
                jnp.zeros((6, width), jnp.float32),
            ],
            axis=0,
        )

    def sd_copy(o):
        return remote(part, part_in.at[o], sd_s.at[o], sd_r.at[o], (lax.rem(d + o, n_dom), z))

    @pl.loop(1, n_dom)
    def _(o):
        sd_copy(o).start()

    part_in[0] = part[...]

    @pl.loop(1, n_dom)
    def _(o):
        sd_copy(o).wait()

    colpart[...] = jnp.sum(part_in[...], axis=0)

    def sc_copy(o):
        q = lax.rem(z + o, n_col)
        return remote(colpart.at[q], colpart_in.at[o], sc_s.at[o - 1], sc_r.at[o - 1], (d, q))

    for o in range(1, n_col):
        sc_copy(o).start()
    colpart_in[0] = colpart[z]

    for o in range(1, n_col):
        w_copy(o).wait_send()

    @pl.loop(1, n_dom)
    def _(o):
        w_pass(o).wait_send()
        for c in range(n_part):
            halo_arrived(c, lax.rem(d + o, n_dom)).wait_send()

    @pl.loop(0, steps)
    def _(s):
        for c in range(n_part):
            for o in range(1, n_col):
                p1_copy(c, s, o).wait_send()

    for o in range(1, n_col):
        sc_copy(o).wait()
    totals = jnp.sum(colpart_in[...], axis=0) / node_total
    mean = totals[0:1, :]
    stat_ref[...] = jnp.concatenate([mean, totals[1:2, :] - mean * mean], axis=0)

    @pl.loop(0, steps * halves)
    def _(s):
        for o in range(1, n_col):
            p2_copy(s, o).wait()
        own_copy(s).wait()


def on_device(
    features,
    weight,
    out_bias,
    local_index,
    local_count,
    local_vals,
    halo_index,
    halo_count,
    halo_vals,
    send_rows,
    send_count,
):
    rows, width = features.shape
    n_dom = lax.axis_size("dom")
    n_col = lax.axis_size("col")
    slot_total = send_rows.shape[2]
    f_total = weight.shape[0]
    n_part = width // LANES
    steps = rows // TILE // n_col // P1_TILES
    steps_out = rows // TILE // n_col // P2_TILES
    r_chunk = P1_TILES * TILE
    r_out = P2_TILES * TILE
    pieces = 8 if rows // TILE % 8 == 0 else 1
    any_spec = pl.BlockSpec(memory_space=pl.ANY)
    vmem = pl.BlockSpec(memory_space=pltpu.VMEM)
    smem = pl.BlockSpec(memory_space=pltpu.SMEM)
    bf16, f32 = jnp.bfloat16, jnp.float32
    dma = pltpu.SemaphoreType.DMA
    halo_bytes = 4 * n_dom * slot_total * width
    grant = 44 * 2**20 + 2 * halo_bytes
    held = pltpu.VMEM if grant + 2 * rows * width < 58 * 2**20 else jax.ShapeDtypeStruct
    grant = grant if held is pltpu.VMEM else 67043328
    normalized, stats = pl.pallas_call(
        functools.partial(kernel, n_dom, n_col, rows * n_dom),
        out_shape=(
            held((rows, width), bf16),
            held((2, width), f32),
        ),
        in_specs=[any_spec, any_spec, vmem, smem, smem, any_spec, smem, smem, any_spec, smem, smem],
        out_specs=(any_spec, vmem),
        scratch_shapes=[
            pltpu.VMEM((n_part, rows // TILE, TILE, LANES), bf16),
            pltpu.VMEM((n_part, rows, LANES), f32),
            pltpu.VMEM((slot_total, LANES), f32),
            pltpu.VMEM((n_part, n_dom, slot_total // TILE, TILE, LANES), bf16),
            pltpu.VMEM((n_dom * slot_total // TILE, TILE, LANES), bf16),
            pltpu.VMEM((n_dom * slot_total // TILE, TILE, LANES), bf16),
            pltpu.VMEM(local_vals.shape[1:], bf16),
            pltpu.VMEM(halo_vals.shape[1:], bf16),
            pltpu.VMEM((n_col, n_dom, f_total // n_dom, width), bf16),
            pltpu.VMEM((n_col, 16, width), bf16),
            pltpu.VMEM((n_part, steps, n_col - 1, r_chunk, LANES), bf16),
            pltpu.VMEM((steps, r_chunk, n_col * width), bf16),
            pltpu.VMEM((steps_out, n_col, r_out, width), bf16),
            pltpu.VMEM((n_col, 2, 8, width), f32),
            pltpu.VMEM((n_col, 8, width), f32),
            pltpu.VMEM((n_dom, n_col, 8, width), f32),
            pltpu.VMEM((n_col, 8, width), f32),
            pltpu.VMEM((n_col, 8, width), f32),
            dma((n_part, pieces)),
            dma((2,)),
            dma,
            dma((n_part, n_dom)),
            dma((n_part, n_dom)),
            dma((n_col - 1,)),
            dma((n_col - 1,)),
            dma((n_dom,)),
            dma((n_dom,)),
            dma((n_col - 1,)),
            dma((n_col - 1,)),
            dma((n_part, steps, n_col - 1)),
            dma((n_part, steps, n_col - 1)),
            dma((steps_out, n_col - 1)),
            dma((steps_out, n_col - 1)),
            dma((steps_out,)),
            dma((n_dom,)),
            dma((n_dom,)),
            dma((n_col - 1,)),
            dma((n_col - 1,)),
        ],
        compiler_params=pltpu.CompilerParams(
            collective_id=0, has_side_effects=True, vmem_limit_bytes=grant
        ),
    )(
        features.reshape(rows // TILE, TILE, width),
        weight,
        out_bias.reshape(1, width),
        local_index[0].T,
        local_count,
        local_vals[0],
        halo_index[0].T,
        halo_count,
        halo_vals[0],
        send_rows[0],
        send_count,
    )
    return normalized, stats


def solution(mesh):
    in_specs = (
        P("dom", "col"),
        P(None, "col"),
        P("col"),
        P("dom", None, None),
        P("dom", None),
        P("dom", None, None, None, None),
        P("dom", None, None),
        P("dom", None),
        P("dom", None, None, None, None),
        P("dom", None, None),
        P("dom", None),
    )
    out_specs = (P("dom", "col"), P(None, "col"))
    return jax.shard_map(
        on_device, mesh=mesh, in_specs=in_specs, out_specs=out_specs, check_vma=False
    )
```

time: 227 us -> 218 us (0.960)
  Pallas kernels: 221 us -> 212 us
    pallas_call x1, Pallas kernels: 221 us -> 212 us  [on_device(): pl.pallas_call(functools.partial(kernel, n_dom, n_col, rows * n_dom), out...]
where the time goes in v1:
time: 218 us; the launch traced here: 216 us
  Pallas kernels  212 us (97%)
  local copies, waits for them, and re-layouts  3.81 us (2%)
    pallas_call x1, Pallas kernels, on_device(): pl.pallas_call(functools.partial(kernel, n_dom, n_col, rows * n_dom), out...  212 us

profile of v1, /device:TPU:1, one launch (start us, length us, event | category | flops | bytes accessed | tf_op | source)
XLA Modules:
  0.0 216.2 jit_solution(15532481749526850047)
XLA Ops:
  0.6 1.2 reshape.11.bias_ref
  1.9 211.8 %shard_map.122 = (bf16[8192,256]{1,0:T(8,128)(2,1)S(1)}, f32[2,256]{1,0:T(2,128)S(1)}) custom-call(bf16[64,128,256]{2,1,0:T(8,128)(2,1)} %bitcast.12, bf16[1024,256]{1,0:T(8,128)(2,1)} %weight_hbm.1, bf16[1,256]{1,0:T(2,128)(2,1)} %reshape.11.bias_ref, s32[4,64]{1,0:T(4,128)} %bitcast.14, s32[1,64]{1,0:T(1,128)} %lcnt.1, bf16[64,4,128,128]{3,2,1,0:T(8,128)(2,1)} %bitcast.10, ...), custom_call_target="tpu_custom_call" | custom-call | tf_op jit(solution)/shard_map/pallas_call | solution.py:437
  213.6 2.0 copy.15
  215.7 0.6 copy.16

commit v2 on v1

--- a/solution.py
+++ b/solution.py
@@ -123,44 +123,13 @@
     w_load().start()
     for i in range(pieces):
         feat_copy(1, i).start()
-    bfull[z] = jnp.broadcast_to(bias_ref[...], bfull.shape[1:])
+    bfull[z] = jnp.broadcast_to(bias_ref[...].reshape(1, width), bfull.shape[1:])
 
     barrier = pltpu.get_barrier_semaphore()
     for o in range(1, n_dom):
         pl.semaphore_signal(barrier, inc=1, device_id=(lax.rem(d + o, n_dom), z), device_id_type=MESH)
     for o in range(1, n_col):
         pl.semaphore_signal(barrier, inc=1, device_id=(d, lax.rem(z + o, n_col)), device_id_type=MESH)
-    pl.semaphore_wait(barrier, n_dom - 1 + n_col - 1)
-
-    def w_copy(o):
-        return remote(
-            wfull.at[z, d], wfull.at[z, d], w_s.at[o - 1], w_r.at[o - 1], (d, lax.rem(z + o, n_col))
-        )
-
-    def w_arrived(o):
-        src = lax.rem(z + n_col - o, n_col)
-        return remote(
-            wfull.at[src, d], wfull.at[src, d], w_s.at[o - 1], w_r.at[o - 1], (d, src)
-        )
-
-    def w_pass(o):
-        return remote(
-            wfull.at[:, d], wfull.at[:, d], wp_s.at[o], wp_r.at[o], (lax.rem(d + o, n_dom), z)
-        )
-
-    def w_passed(o):
-        src = lax.rem(d + n_dom - o, n_dom)
-        return remote(wfull.at[:, src], wfull.at[:, src], wp_s.at[o], wp_r.at[o], (src, z))
-
-    def b_copy(o):
-        return remote(
-            bfull.at[z], bfull.at[z], b_s.at[o - 1], b_r.at[o - 1], (d, lax.rem(z + o, n_col))
-        )
-
-    w_load().wait()
-    for o in range(1, n_col):
-        w_copy(o).start()
-        b_copy(o).start()
 
     def widen(c):
         @pl.loop(0, pieces)
@@ -170,6 +139,43 @@
                 t = i * piece + j
                 xf[c, pl.ds(pl.multiple_of(t * TILE, TILE), TILE), :] = xb[c, t].astype(jnp.float32)
 
+    widen(0)
+    lv_copy = pltpu.make_async_copy(lvals_hbm, lvals, vals_sem.at[0])
+    hv_copy = pltpu.make_async_copy(hvals_hbm, hvals, vals_sem.at[1])
+    lv_copy.start()
+    hv_copy.start()
+    pl.semaphore_wait(barrier, n_dom - 1 + n_col - 1)
+
+    def w_copy(o):
+        return remote(
+            wfull.at[z, d], wfull.at[z, d], w_s.at[o - 1], w_r.at[o - 1], (d, lax.rem(z + o, n_col))
+        )
+
+    def w_arrived(o):
+        src = lax.rem(z + n_col - o, n_col)
+        return remote(
+            wfull.at[src, d], wfull.at[src, d], w_s.at[o - 1], w_r.at[o - 1], (d, src)
+        )
+
+    def w_pass(o):
+        return remote(
+            wfull.at[:, d], wfull.at[:, d], wp_s.at[o], wp_r.at[o], (lax.rem(d + o, n_dom), z)
+        )
+
+    def w_passed(o):
+        src = lax.rem(d + n_dom - o, n_dom)
+        return remote(wfull.at[:, src], wfull.at[:, src], wp_s.at[o], wp_r.at[o], (src, z))
+
+    def b_copy(o):
+        return remote(
+            bfull.at[z], bfull.at[z], b_s.at[o - 1], b_r.at[o - 1], (d, lax.rem(z + o, n_col))
+        )
+
+    w_load().wait()
+    for o in range(1, n_col):
+        w_copy(o).start()
+        b_copy(o).start()
+
     def slots_of(q):
         return pl.ds(q * per_peer, per_peer)
 
@@ -192,11 +198,13 @@
         )
 
     def gather(c, peer):
-        @pl.loop(0, slot_total // 16)
+        @pl.loop(0, slot_total // LANES)
         def _(g):
-            for k in range(16):
-                at = g * 16 + k
-                stage[at] = xf[c, srows[peer, at]]
+            group = pl.ds(pl.multiple_of(g * LANES, LANES), LANES)
+            picked = srows.at[:, group]
+            into = stage.at[group]
+            for k in range(LANES):
+                into[k] = xf[c, picked[peer, k]]
 
         used = lax.broadcasted_iota(jnp.int32, (slot_total, lanes), 0) < scnt[0, peer]
         sent = jnp.where(used, stage[...], 0.0).astype(outgoing.dtype)
@@ -204,27 +212,24 @@
         halo_send(c, peer).start()
 
     def gather_all(c):
-        @pl.loop(1, n_chips)
-        def _(j):
-            gather(c, 2 * lax.rem(chip + j, n_chips))
-
-        gather(c, mate)
-
-        @pl.loop(1, n_chips)
-        def _(j):
-            gather(c, 2 * lax.rem(chip + j, n_chips) + 1)
-
-    lv_copy = pltpu.make_async_copy(lvals_hbm, lvals, vals_sem.at[0])
-    hv_copy = pltpu.make_async_copy(hvals_hbm, hvals, vals_sem.at[1])
-
-    widen(0)
-    lv_copy.start()
-    hv_copy.start()
+        @pl.loop(0, n_dom - 1)
+        def _(i):
+            side = i // n_chips
+            at_mate = (i + 1) // n_chips - side
+            over = 2 * lax.rem(chip + lax.rem(i, n_chips) + 1, n_chips) + side
+            gather(c, over + at_mate * (1 - core))
+
+    def zero_own(c):
+        halos[c][slots_of(d)] = jnp.zeros((per_peer, TILE, lanes), halo_a.dtype)
+
     gather_all(0)
     widen(1)
-    gather_all(1)
     for c in range(n_part):
-        halos[c][slots_of(d)] = jnp.zeros((per_peer, TILE, lanes), halo_a.dtype)
+        zero_own(c)
+
+    @pl.when(core == 1)
+    def _():
+        gather_all(1)
 
     lv_copy.wait()
     hv_copy.wait()
@@ -278,6 +283,11 @@
                 rx[s, i * TILE : (i + 1) * TILE, my_cols(c)] = tile_rows(c, z * tiles_q + s * ct + i)
 
         if c == 0:
+
+            @pl.when(core == 0)
+            def _():
+                gather_all(1)
+
             for o in range(1, n_col):
                 w_arrived(o).wait_recv()
 
@@ -488,7 +498,7 @@
     )(
         features.reshape(rows // TILE, TILE, width),
         weight,
-        out_bias.reshape(1, width),
+        out_bias,
         local_index[0].T,
         local_count,
         local_vals[0],

time: 218 us -> 205 us (0.940)
  Pallas kernels: 212 us -> 202 us
    pallas_call x1, Pallas kernels: 212 us -> 202 us  [on_device(): pl.pallas_call(functools.partial(kernel, n_dom, n_col, rows * n_dom), out...]
where the time goes in v2:
time: 205 us
  Pallas kernels  202 us (99%)
  local copies, waits for them, and re-layouts  2.59 us (1%)
    pallas_call x1, Pallas kernels, on_device(): pl.pallas_call(functools.partial(kernel, n_dom, n_col, rows * n_dom), out...  202 us

profile of v2, /device:TPU:1, one launch (start us, length us, event | category | flops | bytes accessed | tf_op | source)
XLA Modules:
  0.0 205.1 jit_solution(5263260728532784085)
XLA Ops:
  0.6 201.8 %shard_map.122 = (bf16[8192,256]{1,0:T(8,128)(2,1)S(1)}, f32[2,256]{1,0:T(2,128)S(1)}) custom-call(bf16[64,128,256]{2,1,0:T(8,128)(2,1)} %bitcast.12, bf16[1024,256]{1,0:T(8,128)(2,1)} %weight_hbm.1, bf16[256]{0:T(256)(128)(2,1)} %bias_ref.1, s32[4,64]{1,0:T(4,128)} %bitcast.14, s32[1,64]{1,0:T(1,128)} %lcnt.1, bf16[64,4,128,128]{3,2,1,0:T(8,128)(2,1)} %bitcast.10, ...), custom_call_target="tpu_custom_call" | custom-call | tf_op jit(solution)/shard_map/pallas_call | solution.py:447
  202.5 2.0 copy.15
  204.5 0.6 copy.16

commit v3 on v2

v3 whole, which is shorter than its diff:
```python
import functools

import jax
import jax.numpy as jnp
from jax import lax
from jax.experimental import pallas as pl
from jax.experimental.pallas import tpu as pltpu
from jax.sharding import PartitionSpec as P

TILE = 128
MESH = pl.DeviceIdType.MESH
LANES = 128
P1_TILES = 4
P2_TILES = 2
epsilon = 1e-06


def remote(src, dst, send_sem, recv_sem, device):
    return pltpu.make_async_remote_copy(
        src_ref=src,
        dst_ref=dst,
        send_sem=send_sem,
        recv_sem=recv_sem,
        device_id=device,
        device_id_type=MESH,
    )


def kernel(
    n_dom,
    n_col,
    node_total,
    feat_hbm,
    weight_hbm,
    bias_ref,
    lidx_hbm,
    lcnt_hbm,
    lvals_hbm,
    hidx_hbm,
    hcnt_hbm,
    hvals_hbm,
    srows_hbm,
    scnt_hbm,
    out_hbm,
    stat_ref,
    xb,
    xf,
    stage,
    outgoing,
    halo_a,
    halo_b,
    lvals,
    hvals,
    wfull,
    bfull,
    tx,
    rx,
    tx2,
    acc,
    part,
    part_in,
    colpart,
    colpart_in,
    lidx,
    lcnt,
    hidx,
    hcnt,
    srows,
    scnt,
    feat_sem,
    late_sem,
    index_sem,
    vals_sem,
    wl_sem,
    halo_s,
    halo_r,
    w_s,
    w_r,
    wp_s,
    wp_r,
    b_s,
    b_r,
    p1_s,
    p1_r,
    p2_s,
    p2_r,
    own_sem,
    sd_s,
    sd_r,
    sc_s,
    sc_r,
):
    d = lax.axis_index("dom")
    z = lax.axis_index("col")
    halos = (halo_a, halo_b)
    n_part, rows, lanes = xf.shape
    width = n_part * lanes
    slot_total = srows.shape[1]
    k_local = lvals.shape[1]
    k_halo = hvals.shape[1]
    f_total = weight_hbm.shape[0]
    tiles_q = rows // TILE // n_col
    rows_q = tiles_q * TILE
    ct = P1_TILES
    r_chunk = ct * TILE
    steps = tiles_q // ct
    r_out = P2_TILES * TILE
    halves = r_chunk // r_out
    per_peer = slot_total // TILE
    shard = f_total // n_dom
    n_chips = n_dom // 2
    chip = d // 2
    core = lax.rem(d, 2)
    mate = d + 1 - 2 * core

    pieces = feat_sem.shape[0]
    piece = rows // TILE // pieces

    def feat_copy(i):
        at = pl.ds(i * piece, piece)
        return pltpu.make_async_copy(
            feat_hbm.at[at, :, pl.ds(0, lanes)], xb.at[0, at], feat_sem.at[i]
        )

    def late_copy():
        return pltpu.make_async_copy(
            feat_hbm.at[:, :, pl.ds(lanes, lanes)], xb.at[1], late_sem
        )

    tables = [
        pltpu.make_async_copy(src, dst, index_sem.at[i])
        for i, (src, dst) in enumerate(
            (
                (srows_hbm, srows),
                (scnt_hbm, scnt),
                (lidx_hbm, lidx),
                (lcnt_hbm, lcnt),
                (hidx_hbm, hidx),
                (hcnt_hbm, hcnt),
            )
        )
    ]

    def w_load():
        mine = pl.ds(pl.multiple_of(d * shard, shard), shard)
        return pltpu.make_async_copy(weight_hbm.at[mine], wfull.at[z, d], wl_sem)

    for copy in tables[:2]:
        copy.start()
    for i in range(pieces):
        feat_copy(i).start()
    w_load().start()
    late_copy().start()
    for copy in tables[2:]:
        copy.start()

    barrier = pltpu.get_barrier_semaphore()
    for o in range(1, n_dom):
        pl.semaphore_signal(barrier, inc=1, device_id=(lax.rem(d + o, n_dom), z), device_id_type=MESH)
    for o in range(1, n_col):
        pl.semaphore_signal(barrier, inc=1, device_id=(d, lax.rem(z + o, n_col)), device_id_type=MESH)
    bfull[z] = jnp.broadcast_to(bias_ref[...].reshape(1, width), bfull.shape[1:])

    def widen(c, t):
        xf[c, pl.ds(pl.multiple_of(t * TILE, TILE), TILE), :] = xb[c, t].astype(jnp.float32)

    @pl.loop(0, pieces)
    def _(i):
        feat_copy(i).wait()
        for j in range(piece):
            widen(0, i * piece + j)

    def widen_late():
        late_copy().wait()

        @pl.loop(0, pieces)
        def _(i):
            for j in range(piece):
                widen(1, i * piece + j)

    def peer_of(i):
        side = i // n_chips
        at_mate = (i + 1) // n_chips - side
        over = 2 * lax.rem(chip + lax.rem(i, n_chips) + 1, n_chips) + side
        return over + at_mate * (1 - core)

    def slots_of(q):
        return pl.ds(q * per_peer, per_peer)

    def halo_send(c, peer):
        return remote(
            outgoing.at[c, peer],
            halos[c].at[slots_of(d)],
            halo_s.at[c],
            halo_r.at[c],
            (peer, z),
        )

    def halo_all(c):
        most = pl.ds(0, n_dom - 1)
        return remote(
            outgoing.at[c, most],
            outgoing.at[c, most],
            halo_s.at[c],
            halo_r.at[c],
            (mate, z),
        )

    def gather(c, peer):
        @pl.loop(0, slot_total // LANES)
        def _(g):
            group = pl.ds(pl.multiple_of(g * LANES, LANES), LANES)
            picked = srows.at[:, group]
            into = stage.at[group]
            for k in range(LANES):
                into[k] = xf[c, picked[peer, k]]

        used = lax.broadcasted_iota(jnp.int32, (slot_total, lanes), 0) < scnt[0, peer]
        sent = jnp.where(used, stage[...], 0.0).astype(outgoing.dtype)
        outgoing[c, peer] = sent.reshape(per_peer, TILE, lanes)

    def gather_all(c, first):
        @pl.loop(first, n_dom - 1)
        def _(i):
            gather(c, peer_of(i))
            halo_send(c, peer_of(i)).start()

    for copy in tables[:2]:
        copy.wait()
    gather(0, peer_of(0))
    lv_copy = pltpu.make_async_copy(lvals_hbm, lvals, vals_sem.at[0])
    hv_copy = pltpu.make_async_copy(hvals_hbm, hvals, vals_sem.at[1])
    lv_copy.start()
    hv_copy.start()
    pl.semaphore_wait(barrier, n_dom - 1 + n_col - 1)
    halo_send(0, peer_of(0)).start()

    def w_copy(o):
        return remote(wfull.at[z, d], wfull.at[z, d], w_s, w_r, (d, lax.rem(z + o, n_col)))

    def w_copies():
        some = pl.ds(0, n_col - 1)
        return remote(wfull.at[some, d], wfull.at[some, d], w_s, w_r, (d, lax.rem(z + 1, n_col)))

    def w_pass(o):
        return remote(wfull.at[:, d], wfull.at[:, d], wp_s, wp_r, (lax.rem(d + o, n_dom), z))

    def w_passes():
        most = pl.ds(0, n_dom - 1)
        return remote(wfull.at[:, most], wfull.at[:, most], wp_s, wp_r, (mate, z))

    def b_copy(o):
        return remote(bfull.at[z], bfull.at[z], b_s, b_r, (d, lax.rem(z + o, n_col)))

    def b_copies():
        some = bfull.at[pl.ds(0, n_col - 1)]
        return remote(some, some, b_s, b_r, (d, lax.rem(z + 1, n_col)))

    w_load().wait()
    for o in range(1, n_col):
        w_copy(o).start()
        b_copy(o).start()

    def zero_own(c):
        halos[c][slots_of(d)] = jnp.zeros((per_peer, TILE, lanes), halo_a.dtype)

    gather_all(0, 1)
    widen_late()
    for c in range(n_part):
        zero_own(c)

    @pl.when(core == 1)
    def _():
        gather_all(1, 0)

    for copy in tables[2:]:
        copy.wait()
    lv_copy.wait()
    hv_copy.wait()

    def kept(count, k):
        one = jnp.minimum(jnp.maximum(count - k, 0), 1).astype(jnp.float32)
        return jnp.broadcast_to(one, (TILE, TILE)).astype(jnp.bfloat16)

    def tile_rows(c, t):
        lhs, rhs = [], []
        n_loc, n_hal = lcnt[0, t], hcnt[0, t]
        for k in range(k_local):
            lhs.append(lvals[t, k] * kept(n_loc, k))
            rhs.append(xb[c, lidx[k, t]])
        for k in range(k_halo):
            lhs.append(hvals[t, k] * kept(n_hal, k))
            rhs.append(halos[c][hidx[k, t]])
        total = jnp.dot(
            jnp.concatenate(lhs, axis=1),
            jnp.concatenate(rhs, axis=0),
            preferred_element_type=jnp.float32,
        )
        return total.astype(jnp.bfloat16)

    def p1_copy(c, s, o):
        return remote(
            tx.at[s, o - 1, c], rx.at[s, z, c], p1_s, p1_r.at[s], (d, lax.rem(z + o, n_col))
        )

    def p1_step(s):
        whole = tx.at[s]
        return remote(whole, whole, p1_s, p1_r.at[s], (d, lax.rem(z + 1, n_col)))

    for c in range(n_part):

        halo_all(c).wait_recv()

        @pl.loop(0, steps)
        def _(s):
            for o in range(1, n_col):
                q = lax.rem(z + o, n_col)
                for i in range(ct):
                    tx[s, o - 1, c, i * TILE : (i + 1) * TILE, :] = tile_rows(c, q * tiles_q + s * ct + i)
                p1_copy(c, s, o).start()
            for i in range(ct):
                rx[s, z, c, i * TILE : (i + 1) * TILE, :] = tile_rows(c, z * tiles_q + s * ct + i)

        if c == 0:

            @pl.when(core == 0)
            def _():
                gather_all(1, 0)

            w_copies().wait_recv()

            @pl.loop(1, n_dom)
            def _(o):
                w_pass(o).start()

    w_passes().wait_recv()
    b_copies().wait()

    acc[...] = jnp.zeros_like(acc)

    def out_rows(s):
        return pl.ds(pl.multiple_of(z * rows_q + s * r_out, r_out), r_out)

    def p2_copy(s, o):
        q = lax.rem(z + o, n_col)
        return remote(tx2.at[s, q], out_hbm.at[out_rows(s)], p2_s, p2_r, (d, q))

    def p2_all():
        most = tx2.at[:, pl.ds(0, n_col - 1)]
        return remote(most, most, p2_s, p2_r, (d, lax.rem(z + 1, n_col)))

    def own_copy(s):
        return pltpu.make_async_copy(tx2.at[s, z], out_hbm.at[out_rows(s)], own_sem)

    def own_all():
        mine = tx2.at[:, z]
        return pltpu.make_async_copy(mine, mine, own_sem)

    @pl.loop(0, steps)
    def _(s):
        p1_step(s).wait_recv()

        @pl.loop(0, halves)
        def _(h):
            k = s * halves + h
            at = pl.ds(pl.multiple_of(h * r_out, r_out), r_out)
            mixed = jnp.concatenate(
                [rx[s, j, c, at, :] for j in range(n_col) for c in range(n_part)], axis=1
            )
            power = jnp.zeros((r_out, 1), jnp.float32)
            active = []
            for j in range(n_col):
                y = jnp.dot(
                    mixed, wfull[j].reshape(f_total, width), preferred_element_type=jnp.float32
                )
                y = jnp.maximum(y + bfull[j][0:1, :].astype(jnp.float32), 0.0)
                power = power + jnp.sum(y * y, axis=1, keepdims=True)
                active.append(y)
            factor = lax.rsqrt(power / f_total + epsilon)
            for j in range(n_col):
                scaled = active[j] * factor
                tx2[k, j] = scaled.astype(jnp.bfloat16)
                grouped = scaled.reshape(r_out // 8, 8, width)
                acc[j, 0] += jnp.sum(grouped, axis=0)
                acc[j, 1] += jnp.sum(grouped * grouped, axis=0)
            for o in range(1, n_col):
                p2_copy(k, o).start()
            own_copy(k).start()

    for j in range(n_col):
        part[j] = jnp.concatenate(
            [
                jnp.sum(acc[j, 0], axis=0, keepdims=True),
                jnp.sum(acc[j, 1], axis=0, keepdims=True),
                jnp.zeros((6, width), jnp.float32),
            ],
            axis=0,
        )

    def sd_copy(o):
        return remote(part, part_in.at[o], sd_s, sd_r, (lax.rem(d + o, n_dom), z))

    def sd_all():
        most = part_in.at[pl.ds(1, n_dom - 1)]
        return remote(most, most, sd_s, sd_r, (mate, z))

    @pl.loop(1, n_dom)
    def _(o):
        sd_copy(o).start()

    part_in[0] = part[...]
    sd_all().wait()
    colpart[...] = jnp.sum(part_in[...], axis=0)

    def sc_copy(o):
        q = lax.rem(z + o, n_col)
        return remote(colpart.at[q], colpart_in.at[o], sc_s, sc_r, (d, q))

    def sc_all():
        some = colpart_in.at[pl.ds(1, n_col - 1)]
        return remote(some, some, sc_s, sc_r, (d, lax.rem(z + 1, n_col)))

    for o in range(1, n_col):
        sc_copy(o).start()
    colpart_in[0] = colpart[z]

    w_copies().wait_send()
    w_passes().wait_send()
    for c in range(n_part):
        halo_all(c).wait_send()

    remote(tx, tx, p1_s, p1_r.at[0], (d, lax.rem(z + 1, n_col))).wait_send()
    sc_all().wait()
    totals = jnp.sum(colpart_in[...], axis=0) / node_total
    mean = totals[0:1, :]
    stat_ref[...] = jnp.concatenate([mean, totals[1:2, :] - mean * mean], axis=0)

    p2_all().wait()
    own_all().wait()


def on_device(
    features,
    weight,
    out_bias,
    local_index,
    local_count,
    local_vals,
    halo_index,
    halo_count,
    halo_vals,
    send_rows,
    send_count,
):
    rows, width = features.shape
    n_dom = lax.axis_size("dom")
    n_col = lax.axis_size("col")
    slot_total = send_rows.shape[2]
    f_total = weight.shape[0]
    n_part = width // LANES
    steps = rows // TILE // n_col // P1_TILES
    steps_out = rows // TILE // n_col // P2_TILES
    r_chunk = P1_TILES * TILE
    r_out = P2_TILES * TILE
    pieces = 8 if rows // TILE % 8 == 0 else 1
    any_spec = pl.BlockSpec(memory_space=pl.ANY)
    vmem = pl.BlockSpec(memory_space=pltpu.VMEM)
    bf16, f32 = jnp.bfloat16, jnp.float32
    dma = pltpu.SemaphoreType.DMA

    def table(*shape):
        return pltpu.SMEM(shape, jnp.int32)

    halo_bytes = 4 * n_dom * slot_total * width
    grant = 44 * 2**20 + 2 * halo_bytes
    held = pltpu.VMEM if grant + 2 * rows * width < 58 * 2**20 else jax.ShapeDtypeStruct
    grant = grant if held is pltpu.VMEM else 67043328
    normalized, stats = pl.pallas_call(
        functools.partial(kernel, n_dom, n_col, rows * n_dom),
        out_shape=(
            held((rows, width), bf16),
            held((2, width), f32),
        ),
        in_specs=[any_spec, any_spec, vmem] + [any_spec] * 8,
        out_specs=(any_spec, vmem),
        scratch_shapes=[
            pltpu.VMEM((n_part, rows // TILE, TILE, LANES), bf16),
            pltpu.VMEM((n_part, rows, LANES), f32),
            pltpu.VMEM((slot_total, LANES), f32),
            pltpu.VMEM((n_part, n_dom, slot_total // TILE, TILE, LANES), bf16),
            pltpu.VMEM((n_dom * slot_total // TILE, TILE, LANES), bf16),
            pltpu.VMEM((n_dom * slot_total // TILE, TILE, LANES), bf16),
            pltpu.VMEM(local_vals.shape[1:], bf16),
            pltpu.VMEM(halo_vals.shape[1:], bf16),
            pltpu.VMEM((n_col, n_dom, f_total // n_dom, width), bf16),
            pltpu.VMEM((n_col, 16, width), bf16),
            pltpu.VMEM((steps, n_col - 1, n_part, r_chunk, LANES), bf16),
            pltpu.VMEM((steps, n_col, n_part, r_chunk, LANES), bf16),
            pltpu.VMEM((steps_out, n_col, r_out, width), bf16),
            pltpu.VMEM((n_col, 2, 8, width), f32),
            pltpu.VMEM((n_col, 8, width), f32),
            pltpu.VMEM((n_dom, n_col, 8, width), f32),
            pltpu.VMEM((n_col, 8, width), f32),
            pltpu.VMEM((n_col, 8, width), f32),
            table(local_index.shape[2], rows // TILE),
            table(1, rows // TILE),
            table(halo_index.shape[2], rows // TILE),
            table(1, rows // TILE),
            table(n_dom, slot_total),
            table(1, n_dom),
            dma((pieces,)),
            dma,
            dma((6,)),
            dma((2,)),
            dma,
            dma((n_part,)),
            dma((n_part,)),
            dma,
            dma,
            dma,
            dma,
            dma,
            dma,
            dma,
            dma((steps,)),
            dma,
            dma,
            dma,
            dma,
            dma,
            dma,
            dma,
        ],
        compiler_params=pltpu.CompilerParams(
            collective_id=0, has_side_effects=True, vmem_limit_bytes=grant
        ),
    )(
        features.reshape(rows // TILE, TILE, width),
        weight,
        out_bias,
        local_index[0].T,
        local_count,
        local_vals[0],
        halo_index[0].T,
        halo_count,
        halo_vals[0],
        send_rows[0],
        send_count,
    )
    return normalized, stats


def solution(mesh):
    in_specs = (
        P("dom", "col"),
        P(None, "col"),
        P("col"),
        P("dom", None, None),
        P("dom", None),
        P("dom", None, None, None, None),
        P("dom", None, None),
        P("dom", None),
        P("dom", None, None, None, None),
        P("dom", None, None),
        P("dom", None),
    )
    out_specs = (P("dom", "col"), P(None, "col"))
    return jax.shard_map(
        on_device, mesh=mesh, in_specs=in_specs, out_specs=out_specs, check_vma=False
    )
```

time: 205 us -> 203 us (level)
  Pallas kernels: 202 us -> 199 us
    pallas_call x1, Pallas kernels: 202 us -> 199 us  [on_device(): pl.pallas_call(functools.partial(kernel, n_dom, n_col, rows * n_dom), out...]
where the time goes in v3:
time: 203 us; the launch traced here: 202 us
  Pallas kernels  199 us (98%)
  local copies, waits for them, and re-layouts  2.59 us (1%)
    pallas_call x1, Pallas kernels, on_device(): pl.pallas_call(functools.partial(kernel, n_dom, n_col, rows * n_dom), out...  199 us

profile of v3, /device:TPU:1, one launch (start us, length us, event | category | flops | bytes accessed | tf_op | source)
XLA Modules:
  0.0 202.4 jit_solution(1458570381575516278)
XLA Ops:
  0.6 199.2 %shard_map.122 = (bf16[8192,256]{1,0:T(8,128)(2,1)S(1)}, f32[2,256]{1,0:T(2,128)S(1)}) custom-call(bf16[64,128,256]{2,1,0:T(8,128)(2,1)} %bitcast.12, bf16[1024,256]{1,0:T(8,128)(2,1)} %weight_hbm.1, bf16[256]{0:T(256)(128)(2,1)} %bias_ref.1, s32[4,64]{1,0:T(4,128)} %bitcast.14, s32[1,64]{1,0:T(1,128)} %lcnt_hbm.1, bf16[64,4,128,128]{3,2,1,0:T(8,128)(2,1)} %bitcast.10, ...), custom_call_target="tpu_custom_call" | custom-call | tf_op jit(solution)/shard_map/pallas_call | solution.py:478
  199.9 2.0 copy.15
  201.9 0.6 copy.16

commit v4 on v3

--- a/solution.py
+++ b/solution.py
@@ -12,6 +12,7 @@
 LANES = 128
 P1_TILES = 4
 P2_TILES = 2
+EARLY_STEPS = 1
 epsilon = 1e-06
 
 
@@ -46,9 +47,13 @@
     xb,
     xf,
     stage,
-    outgoing,
-    halo_a,
-    halo_b,
+    out_a,
+    out_b,
+    out_late,
+    land_a,
+    land_b,
+    halo_early,
+    halo_late,
     lvals,
     hvals,
     wfull,
@@ -92,7 +97,9 @@
 ):
     d = lax.axis_index("dom")
     z = lax.axis_index("col")
-    halos = (halo_a, halo_b)
+    halos = (halo_early, halo_late)
+    outs = (out_a, out_b, out_late)
+    lands = (land_a, land_b, halo_late)
     n_part, rows, lanes = xf.shape
     width = n_part * lanes
     slot_total = srows.shape[1]
@@ -107,6 +114,7 @@
     r_out = P2_TILES * TILE
     halves = r_chunk // r_out
     per_peer = slot_total // TILE
+    half_peer = per_peer // 2
     shard = f_total // n_dom
     n_chips = n_dom // 2
     chip = d // 2
@@ -184,29 +192,34 @@
         over = 2 * lax.rem(chip + lax.rem(i, n_chips) + 1, n_chips) + side
         return over + at_mate * (1 - core)
 
-    def slots_of(q):
-        return pl.ds(q * per_peer, per_peer)
-
-    def halo_send(c, peer):
+    def slots_of(k, q):
+        count = outs[k].shape[1]
+        return pl.ds(q * count, count)
+
+    def halo_send(k, peer):
         return remote(
-            outgoing.at[c, peer],
-            halos[c].at[slots_of(d)],
-            halo_s.at[c],
-            halo_r.at[c],
-            (peer, z),
-        )
-
-    def halo_all(c):
-        most = pl.ds(0, n_dom - 1)
-        return remote(
-            outgoing.at[c, most],
-            outgoing.at[c, most],
-            halo_s.at[c],
-            halo_r.at[c],
-            (mate, z),
-        )
-
-    def gather(c, peer):
+            outs[k].at[peer], lands[k].at[slots_of(k, d)], halo_s.at[k], halo_r.at[k], (peer, z)
+        )
+
+    def halo_all(k):
+        most = outs[k].at[pl.ds(0, n_dom - 1)]
+        return remote(most, most, halo_s.at[k], halo_r.at[k], (mate, z))
+
+    def first_lanes(shape):
+        return lax.broadcasted_iota(jnp.int32, shape, len(shape) - 1) < lanes // 2
+
+    def swap(x):
+        return pltpu.roll(x, lanes // 2, x.ndim - 1)
+
+    def fold(low, high):
+        first, turned = first_lanes(low.shape), swap(high)
+        return jnp.where(first, low, turned), jnp.where(first, turned, low)
+
+    def unfold(a, b):
+        first = first_lanes(a.shape)
+        return jnp.where(first, a, b), swap(jnp.where(first, b, a))
+
+    def picked_rows(c, peer):
         @pl.loop(0, slot_total // LANES)
         def _(g):
             group = pl.ds(pl.multiple_of(g * LANES, LANES), LANES)
@@ -216,18 +229,25 @@
                 into[k] = xf[c, picked[peer, k]]
 
         used = lax.broadcasted_iota(jnp.int32, (slot_total, lanes), 0) < scnt[0, peer]
-        sent = jnp.where(used, stage[...], 0.0).astype(outgoing.dtype)
-        outgoing[c, peer] = sent.reshape(per_peer, TILE, lanes)
-
-    def gather_all(c, first):
-        @pl.loop(first, n_dom - 1)
+        return jnp.where(used, stage[...], 0.0)
+
+    def gather_early(peer):
+        sent = picked_rows(0, peer)
+        a, b = fold(sent[: slot_total // 2], sent[slot_total // 2 :])
+        out_a[peer] = a.astype(out_a.dtype).reshape(half_peer, TILE, lanes)
+        out_b[peer] = b.astype(out_b.dtype).reshape(half_peer, TILE, lanes)
+
+    def gather_late():
+        @pl.loop(0, n_dom - 1)
         def _(i):
-            gather(c, peer_of(i))
-            halo_send(c, peer_of(i)).start()
+            peer = peer_of(i)
+            sent = picked_rows(1, peer)
+            out_late[peer] = sent.astype(out_late.dtype).reshape(per_peer, TILE, lanes)
+            halo_send(2, peer).start()
 
     for copy in tables[:2]:
         copy.wait()
-    gather(0, peer_of(0))
+    gather_early(peer_of(0))
     lv_copy = pltpu.make_async_copy(lvals_hbm, lvals, vals_sem.at[0])
     hv_copy = pltpu.make_async_copy(hvals_hbm, hvals, vals_sem.at[1])
     lv_copy.start()
@@ -235,6 +255,15 @@
     pl.semaphore_wait(barrier, n_dom - 1 + n_col - 1)
     halo_send(0, peer_of(0)).start()
 
+    @pl.loop(1, n_chips - 1)
+    def _(i):
+        gather_early(peer_of(i))
+        halo_send(0, peer_of(i)).start()
+
+    @pl.loop(0, n_chips - 1)
+    def _(i):
+        halo_send(1, peer_of(i)).start()
+
     def w_copy(o):
         return remote(wfull.at[z, d], wfull.at[z, d], w_s, w_r, (d, lax.rem(z + o, n_col)))
 
@@ -261,17 +290,20 @@
         w_copy(o).start()
         b_copy(o).start()
 
-    def zero_own(c):
-        halos[c][slots_of(d)] = jnp.zeros((per_peer, TILE, lanes), halo_a.dtype)
-
-    gather_all(0, 1)
+    @pl.loop(n_chips - 1, n_dom - 1)
+    def _(i):
+        gather_early(peer_of(i))
+        halo_send(0, peer_of(i)).start()
+        halo_send(1, peer_of(i)).start()
+
     widen_late()
-    for c in range(n_part):
-        zero_own(c)
+    for k in range(3):
+        mine = slots_of(k, d)
+        lands[k][mine] = jnp.zeros((outs[k].shape[1], TILE, lanes), halo_late.dtype)
 
     @pl.when(core == 1)
     def _():
-        gather_all(1, 0)
+        gather_late()
 
     for copy in tables[2:]:
         copy.wait()
@@ -291,12 +323,11 @@
         for k in range(k_halo):
             lhs.append(hvals[t, k] * kept(n_hal, k))
             rhs.append(halos[c][hidx[k, t]])
-        total = jnp.dot(
+        return jnp.dot(
             jnp.concatenate(lhs, axis=1),
             jnp.concatenate(rhs, axis=0),
             preferred_element_type=jnp.float32,
         )
-        return total.astype(jnp.bfloat16)
 
     def p1_copy(c, s, o):
         return remote(
@@ -307,31 +338,97 @@
         whole = tx.at[s]
         return remote(whole, whole, p1_s, p1_r.at[s], (d, lax.rem(z + 1, n_col)))
 
-    for c in range(n_part):
-
-        halo_all(c).wait_recv()
-
-        @pl.loop(0, steps)
-        def _(s):
-            for o in range(1, n_col):
-                q = lax.rem(z + o, n_col)
-                for i in range(ct):
-                    tx[s, o - 1, c, i * TILE : (i + 1) * TILE, :] = tile_rows(c, q * tiles_q + s * ct + i)
-                p1_copy(c, s, o).start()
+    def p1_part(s, o, k):
+        at = pl.ds(k * (r_chunk // 2), r_chunk // 2)
+        return remote(
+            tx.at[s, o - 1, 0, at],
+            rx.at[s, z, 0, at],
+            p1_s,
+            p1_r.at[s],
+            (d, lax.rem(z + o, n_col)),
+        )
+
+    def folded(s, q, k):
+        tiles = [tile_rows(0, q * tiles_q + s * ct + i) for i in range(ct)]
+        pairs = [fold(tiles[i], tiles[i + ct // 2])[k] for i in range(ct // 2)]
+        return jnp.concatenate(pairs, axis=0).astype(jnp.bfloat16)
+
+    def early_step(s, k):
+        at = pl.ds(k * (r_chunk // 2), r_chunk // 2)
+        for o in range(1, n_col):
+            tx[s, o - 1, 0, at, :] = folded(s, lax.rem(z + o, n_col), k)
+            p1_part(s, o, k).start()
+
+    def own_step(s):
+        for k in range(2):
+            at = pl.ds(k * (r_chunk // 2), r_chunk // 2)
+            rx[s, z, 0, at, :] = folded(s, z, k)
+
+    def full_step(c, s):
+        for o in range(1, n_col):
+            q = lax.rem(z + o, n_col)
             for i in range(ct):
-                rx[s, z, c, i * TILE : (i + 1) * TILE, :] = tile_rows(c, z * tiles_q + s * ct + i)
-
-        if c == 0:
-
-            @pl.when(core == 0)
-            def _():
-                gather_all(1, 0)
-
-            w_copies().wait_recv()
-
-            @pl.loop(1, n_dom)
-            def _(o):
-                w_pass(o).start()
+                rows_i = tile_rows(c, q * tiles_q + s * ct + i)
+                tx[s, o - 1, c, i * TILE : (i + 1) * TILE, :] = rows_i.astype(jnp.bfloat16)
+            p1_copy(c, s, o).start()
+        for i in range(ct):
+            rows_i = tile_rows(c, z * tiles_q + s * ct + i)
+            rx[s, z, c, i * TILE : (i + 1) * TILE, :] = rows_i.astype(jnp.bfloat16)
+
+    def halves_of(land, q):
+        return land[slots_of(0, q)].astype(jnp.float32)
+
+    def place(q, k, tiles):
+        at = pl.ds(q * per_peer + k * half_peer, half_peer)
+        halo_early[at] = tiles.astype(halo_early.dtype)
+
+    halo_all(0).wait_recv()
+
+    @pl.loop(0, n_dom)
+    def _(q):
+        a = halves_of(land_a, q)
+        place(q, 0, a)
+        place(q, 1, swap(a))
+
+    @pl.loop(0, EARLY_STEPS)
+    def _(s):
+        early_step(s, 0)
+
+    halo_all(1).wait_recv()
+
+    @pl.loop(0, n_dom)
+    def _(q):
+        low, high = unfold(halves_of(land_a, q), halves_of(land_b, q))
+        place(q, 0, low)
+        place(q, 1, high)
+
+    @pl.loop(0, EARLY_STEPS)
+    def _(s):
+        early_step(s, 1)
+
+    @pl.loop(EARLY_STEPS, steps)
+    def _(s):
+        full_step(0, s)
+
+    @pl.loop(0, EARLY_STEPS)
+    def _(s):
+        own_step(s)
+
+    @pl.when(core == 0)
+    def _():
+        gather_late()
+
+    w_copies().wait_recv()
+
+    @pl.loop(1, n_dom)
+    def _(o):
+        w_pass(o).start()
+
+    halo_all(2).wait_recv()
+
+    @pl.loop(0, steps)
+    def _(s):
+        full_step(1, s)
 
     w_passes().wait_recv()
     b_copies().wait()
@@ -359,6 +456,15 @@
     @pl.loop(0, steps)
     def _(s):
         p1_step(s).wait_recv()
+
+        @pl.when(s < EARLY_STEPS)
+        def _():
+            for j in range(n_col):
+                a = rx[s, j, 0, : r_chunk // 2, :].astype(jnp.float32)
+                b = rx[s, j, 0, r_chunk // 2 :, :].astype(jnp.float32)
+                low, high = unfold(a, b)
+                rx[s, j, 0, : r_chunk // 2, :] = low.astype(jnp.bfloat16)
+                rx[s, j, 0, r_chunk // 2 :, :] = high.astype(jnp.bfloat16)
 
         @pl.loop(0, halves)
         def _(h):
@@ -426,8 +532,8 @@
 
     w_copies().wait_send()
     w_passes().wait_send()
-    for c in range(n_part):
-        halo_all(c).wait_send()
+    for k in range(3):
+        halo_all(k).wait_send()
 
     remote(tx, tx, p1_s, p1_r.at[0], (d, lax.rem(z + 1, n_col))).wait_send()
     sc_all().wait()
@@ -487,7 +593,11 @@
             pltpu.VMEM((n_part, rows // TILE, TILE, LANES), bf16),
             pltpu.VMEM((n_part, rows, LANES), f32),
             pltpu.VMEM((slot_total, LANES), f32),
-            pltpu.VMEM((n_part, n_dom, slot_total // TILE, TILE, LANES), bf16),
+            pltpu.VMEM((n_dom, slot_total // TILE // 2, TILE, LANES), bf16),
+            pltpu.VMEM((n_dom, slot_total // TILE // 2, TILE, LANES), bf16),
+            pltpu.VMEM((n_dom, slot_total // TILE, TILE, LANES), bf16),
+            pltpu.VMEM((n_dom * slot_total // TILE // 2, TILE, LANES), bf16),
+            pltpu.VMEM((n_dom * slot_total // TILE // 2, TILE, LANES), bf16),
             pltpu.VMEM((n_dom * slot_total // TILE, TILE, LANES), bf16),
             pltpu.VMEM((n_dom * slot_total // TILE, TILE, LANES), bf16),
             pltpu.VMEM(local_vals.shape[1:], bf16),
@@ -513,8 +623,8 @@
             dma((6,)),
             dma((2,)),
             dma,
-            dma((n_part,)),
-            dma((n_part,)),
+            dma((3,)),
+            dma((3,)),
             dma,
             dma,
             dma,

time: 203 us -> 201 us (level)
    pallas_call x1, Pallas kernels: 199 us -> 197 us  [on_device(): pl.pallas_call(functools.partial(kernel, n_dom, n_col, rows * n_dom), out...]
where the time goes in v4:
time: 201 us; the launch traced here: 200 us
  Pallas kernels  197 us (98%)
  local copies, waits for them, and re-layouts  2.59 us (1%)
    pallas_call x1, Pallas kernels, on_device(): pl.pallas_call(functools.partial(kernel, n_dom, n_col, rows * n_dom), out...  197 us

profile of v4, /device:TPU:1, one launch (start us, length us, event | category | flops | bytes accessed | tf_op | source)
XLA Modules:
  0.0 200.4 jit_solution(6833487179185051566)
XLA Ops:
  0.6 197.2 %shard_map.122 = (bf16[8192,256]{1,0:T(8,128)(2,1)S(1)}, f32[2,256]{1,0:T(2,128)S(1)}) custom-call(bf16[64,128,256]{2,1,0:T(8,128)(2,1)} %bitcast.12, bf16[1024,256]{1,0:T(8,128)(2,1)} %weight_hbm.1, bf16[256]{0:T(256)(128)(2,1)} %bias_ref.1, s32[4,64]{1,0:T(4,128)} %bitcast.14, s32[1,64]{1,0:T(1,128)} %lcnt_hbm.1, bf16[64,4,128,128]{3,2,1,0:T(8,128)(2,1)} %bitcast.10, ...), custom_call_target="tpu_custom_call" | custom-call | tf_op jit(solution)/shard_map/pallas_call | solution.py:584
  197.8 2.0 %copy.15 = bf16[8192,256]{1,0:T(8,128)(2,1)} copy(bf16[8192,256]{1,0:T(8,128)(2,1)S(1)} %get-tuple-element.2) | data formatting | bytes 8388608
  199.8 0.6 copy.16

commit v5 on v4

--- a/solution.py
+++ b/solution.py
@@ -44,7 +44,8 @@
     scnt_hbm,
     out_hbm,
     stat_ref,
-    xb,
+    xb_early,
+    xb_late,
     xf,
     stage,
     out_a,
@@ -98,11 +99,12 @@
     d = lax.axis_index("dom")
     z = lax.axis_index("col")
     halos = (halo_early, halo_late)
+    xb = (xb_early, xb_late)
     outs = (out_a, out_b, out_late)
     lands = (land_a, land_b, halo_late)
     n_part, rows, lanes = xf.shape
     width = n_part * lanes
-    slot_total = srows.shape[1]
+    slot_total = srows_hbm.shape[1]
     k_local = lvals.shape[1]
     k_halo = hvals.shape[1]
     f_total = weight_hbm.shape[0]
@@ -127,40 +129,35 @@
     def feat_copy(i):
         at = pl.ds(i * piece, piece)
         return pltpu.make_async_copy(
-            feat_hbm.at[at, :, pl.ds(0, lanes)], xb.at[0, at], feat_sem.at[i]
+            feat_hbm.at[at, :, pl.ds(0, lanes)], xb_early.at[at], feat_sem.at[i]
         )
 
     def late_copy():
         return pltpu.make_async_copy(
-            feat_hbm.at[:, :, pl.ds(lanes, lanes)], xb.at[1], late_sem
+            feat_hbm.at[:, :, pl.ds(lanes, lanes)], xb_late, late_sem
         )
 
+    groups = srows.shape[0]
+    pairs = [(srows_hbm.at[:, pl.ds(g * LANES, LANES)], srows.at[g]) for g in range(groups)]
+    pairs += [(scnt_hbm, scnt), (lidx_hbm, lidx), (lcnt_hbm, lcnt), (hidx_hbm, hidx), (hcnt_hbm, hcnt)]
     tables = [
-        pltpu.make_async_copy(src, dst, index_sem.at[i])
-        for i, (src, dst) in enumerate(
-            (
-                (srows_hbm, srows),
-                (scnt_hbm, scnt),
-                (lidx_hbm, lidx),
-                (lcnt_hbm, lcnt),
-                (hidx_hbm, hidx),
-                (hcnt_hbm, hcnt),
-            )
-        )
+        pltpu.make_async_copy(src, dst, index_sem.at[i]) for i, (src, dst) in enumerate(pairs)
     ]
+    first_tables, other_tables = tables[: groups + 1], tables[groups + 1 :]
 
     def w_load():
         mine = pl.ds(pl.multiple_of(d * shard, shard), shard)
         return pltpu.make_async_copy(weight_hbm.at[mine], wfull.at[z, d], wl_sem)
 
-    for copy in tables[:2]:
+    for copy in first_tables:
         copy.start()
     for i in range(pieces):
         feat_copy(i).start()
     w_load().start()
-    late_copy().start()
-    for copy in tables[2:]:
+    for copy in other_tables:
         copy.start()
+    lv_copy = pltpu.make_async_copy(lvals_hbm, lvals, vals_sem.at[0])
+    hv_copy = pltpu.make_async_copy(hvals_hbm, hvals, vals_sem.at[1])
 
     barrier = pltpu.get_barrier_semaphore()
     for o in range(1, n_dom):
@@ -169,8 +166,17 @@
         pl.semaphore_signal(barrier, inc=1, device_id=(d, lax.rem(z + o, n_col)), device_id_type=MESH)
     bfull[z] = jnp.broadcast_to(bias_ref[...].reshape(1, width), bfull.shape[1:])
 
+    def slots_of(k, q):
+        count = outs[k].shape[1]
+        return pl.ds(q * count, count)
+
+    for k in range(3):
+        mine = slots_of(k, d)
+        lands[k][mine] = jnp.zeros((outs[k].shape[1], TILE, lanes), halo_late.dtype)
+    acc[...] = jnp.zeros_like(acc)
+
     def widen(c, t):
-        xf[c, pl.ds(pl.multiple_of(t * TILE, TILE), TILE), :] = xb[c, t].astype(jnp.float32)
+        xf[c, pl.ds(pl.multiple_of(t * TILE, TILE), TILE), :] = xb[c][t].astype(jnp.float32)
 
     @pl.loop(0, pieces)
     def _(i):
@@ -178,6 +184,10 @@
         for j in range(piece):
             widen(0, i * piece + j)
 
+    lv_copy.start()
+    hv_copy.start()
+    late_copy().start()
+
     def widen_late():
         late_copy().wait()
 
@@ -192,10 +202,6 @@
         over = 2 * lax.rem(chip + lax.rem(i, n_chips) + 1, n_chips) + side
         return over + at_mate * (1 - core)
 
-    def slots_of(k, q):
-        count = outs[k].shape[1]
-        return pl.ds(q * count, count)
-
     def halo_send(k, peer):
         return remote(
             outs[k].at[peer], lands[k].at[slots_of(k, d)], halo_s.at[k], halo_r.at[k], (peer, z)
@@ -223,10 +229,9 @@
         @pl.loop(0, slot_total // LANES)
         def _(g):
             group = pl.ds(pl.multiple_of(g * LANES, LANES), LANES)
-            picked = srows.at[:, group]
             into = stage.at[group]
             for k in range(LANES):
-                into[k] = xf[c, picked[peer, k]]
+                into[k] = xf[c, srows[g, peer, k]]
 
         used = lax.broadcasted_iota(jnp.int32, (slot_total, lanes), 0) < scnt[0, peer]
         return jnp.where(used, stage[...], 0.0)
@@ -245,13 +250,9 @@
             out_late[peer] = sent.astype(out_late.dtype).reshape(per_peer, TILE, lanes)
             halo_send(2, peer).start()
 
-    for copy in tables[:2]:
+    for copy in first_tables:
         copy.wait()
     gather_early(peer_of(0))
-    lv_copy = pltpu.make_async_copy(lvals_hbm, lvals, vals_sem.at[0])
-    hv_copy = pltpu.make_async_copy(hvals_hbm, hvals, vals_sem.at[1])
-    lv_copy.start()
-    hv_copy.start()
     pl.semaphore_wait(barrier, n_dom - 1 + n_col - 1)
     halo_send(0, peer_of(0)).start()
 
@@ -296,16 +297,12 @@
         halo_send(0, peer_of(i)).start()
         halo_send(1, peer_of(i)).start()
 
-    widen_late()
-    for k in range(3):
-        mine = slots_of(k, d)
-        lands[k][mine] = jnp.zeros((outs[k].shape[1], TILE, lanes), halo_late.dtype)
-
     @pl.when(core == 1)
     def _():
+        widen_late()
         gather_late()
 
-    for copy in tables[2:]:
+    for copy in other_tables:
         copy.wait()
     lv_copy.wait()
     hv_copy.wait()
@@ -319,7 +316,7 @@
         n_loc, n_hal = lcnt[0, t], hcnt[0, t]
         for k in range(k_local):
             lhs.append(lvals[t, k] * kept(n_loc, k))
-            rhs.append(xb[c, lidx[k, t]])
+            rhs.append(xb[c][lidx[k, t]])
         for k in range(k_halo):
             lhs.append(hvals[t, k] * kept(n_hal, k))
             rhs.append(halos[c][hidx[k, t]])
@@ -416,6 +413,7 @@
 
     @pl.when(core == 0)
     def _():
+        widen_late()
         gather_late()
 
     w_copies().wait_recv()
@@ -432,8 +430,6 @@
 
     w_passes().wait_recv()
     b_copies().wait()
-
-    acc[...] = jnp.zeros_like(acc)
 
     def out_rows(s):
         return pl.ds(pl.multiple_of(z * rows_q + s * r_out, r_out), r_out)
@@ -543,6 +539,17 @@
 
     p2_all().wait()
     own_all().wait()
+
+
+def flush(rows_ref, stat_ref, out_hbm, stat_hbm, row_sem, stat_sem):
+    small = pltpu.make_async_copy(stat_ref, stat_hbm, stat_sem)
+    small.start()
+    piece = out_hbm.shape[0] // 8
+    for i in range(8):
+        at = pl.ds(i * piece, piece)
+        pltpu.make_async_copy(rows_ref.at[at], out_hbm.at[at], row_sem).start()
+    pltpu.make_async_copy(rows_ref, out_hbm, row_sem).wait()
+    small.wait()
 
 
 def on_device(
@@ -590,7 +597,8 @@
         in_specs=[any_spec, any_spec, vmem] + [any_spec] * 8,
         out_specs=(any_spec, vmem),
         scratch_shapes=[
-            pltpu.VMEM((n_part, rows // TILE, TILE, LANES), bf16),
+            pltpu.VMEM((rows // TILE, TILE, LANES), bf16),
+            pltpu.VMEM((rows // TILE, TILE, LANES), bf16),
             pltpu.VMEM((n_part, rows, LANES), f32),
             pltpu.VMEM((slot_total, LANES), f32),
             pltpu.VMEM((n_dom, slot_total // TILE // 2, TILE, LANES), bf16),
@@ -616,11 +624,11 @@
             table(1, rows // TILE),
             table(halo_index.shape[2], rows // TILE),
             table(1, rows // TILE),
-            table(n_dom, slot_total),
+            table(slot_total // LANES, n_dom, LANES),
             table(1, n_dom),
             dma((pieces,)),
             dma,
-            dma((6,)),
+            dma((slot_total // LANES + 5,)),
             dma((2,)),
             dma,
             dma((3,)),
@@ -657,7 +665,19 @@
         send_rows[0],
         send_count,
     )
-    return normalized, stats
+    if held is not pltpu.VMEM:
+        return normalized, stats
+    return pl.pallas_call(
+        flush,
+        out_shape=(
+            jax.ShapeDtypeStruct((rows, width), bf16),
+            jax.ShapeDtypeStruct((2, width), f32),
+        ),
+        in_specs=[vmem, vmem],
+        out_specs=(any_spec, any_spec),
+        scratch_shapes=[dma, dma],
+        compiler_params=pltpu.CompilerParams(vmem_limit_bytes=16 * 2**20),
+    )(normalized, stats)
 
 
 def solution(mesh):

time: 201 us -> 200 us (level)
  local copies, waits for them, and re-layouts: 2.59 us -> 0 us
    unnamed x2 -> x0, local copies, waits for them, and re-layouts: 2.59 us -> none
    pallas_call x0 -> x1, Pallas kernels: none -> 2.02 us  [on_device(): pl.pallas_call(flush, out_shape=(jax.ShapeDtypeStruct((rows, width), bf16...]
where the time goes in v5:
time: 200 us
  Pallas kernels  199 us (100%)
    pallas_call x1, Pallas kernels, on_device(): pl.pallas_call(functools.partial(kernel, n_dom, n_col, rows * n_dom), out...  197 us

profile of v5, /device:TPU:1, one launch (start us, length us, event | category | flops | bytes accessed | tf_op | source)
XLA Modules:
  0.0 199.6 jit_solution(1167064892632045213)
XLA Ops:
  0.6 196.9 %shard_map.122 = (bf16[8192,256]{1,0:T(8,128)(2,1)S(1)}, f32[2,256]{1,0:T(2,128)S(1)}) custom-call(bf16[64,128,256]{2,1,0:T(8,128)(2,1)} %bitcast.12, bf16[1024,256]{1,0:T(8,128)(2,1)} %weight_hbm.1, bf16[256]{0:T(256)(128)(2,1)} %bias_ref.1, s32[4,64]{1,0:T(4,128)} %bitcast.14, s32[1,64]{1,0:T(1,128)} %lcnt_hbm.1, bf16[64,4,128,128]{3,2,1,0:T(8,128)(2,1)} %bitcast.10, ...), custom_call_target="tpu_custom_call" | custom-call | tf_op jit(solution)/shard_map/pallas_call | solution.py:591
  197.6 2.0 %shard_map.123 = (bf16[8192,256]{1,0:T(8,128)(2,1)}, f32[2,256]{1,0:T(2,128)}) custom-call(bf16[8192,256]{1,0:T(8,128)(2,1)S(1)} %get-tuple-element.4.rows_ref, f32[2,256]{1,0:T(2,128)S(1)} %get-tuple-element.5.stat_ref), custom_call_target="tpu_custom_call" | custom-call | tf_op jit(solution)/shard_map/pallas_call | solution.py:670

commit v6 on v5

--- a/solution.py
+++ b/solution.py
@@ -197,10 +197,10 @@
                 widen(1, i * piece + j)
 
     def peer_of(i):
-        side = i // n_chips
-        at_mate = (i + 1) // n_chips - side
-        over = 2 * lax.rem(chip + lax.rem(i, n_chips) + 1, n_chips) + side
-        return over + at_mate * (1 - core)
+        later = i // n_chips
+        at_mate = (i + 1) // n_chips - later
+        over = 2 * lax.rem(chip + lax.rem(i, n_chips) + 1, n_chips) + 1 - later
+        return over - at_mate * core
 
     def halo_send(k, peer):
         return remote(
@@ -250,11 +250,36 @@
             out_late[peer] = sent.astype(out_late.dtype).reshape(per_peer, TILE, lanes)
             halo_send(2, peer).start()
 
+    def w_copy(o):
+        return remote(wfull.at[z, d], wfull.at[z, d], w_s, w_r, (d, lax.rem(z + o, n_col)))
+
+    def w_copies():
+        some = pl.ds(0, n_col - 1)
+        return remote(wfull.at[some, d], wfull.at[some, d], w_s, w_r, (d, lax.rem(z + 1, n_col)))
+
+    def w_pass(o):
+        return remote(wfull.at[:, d], wfull.at[:, d], wp_s, wp_r, (lax.rem(d + o, n_dom), z))
+
+    def w_passes():
+        most = pl.ds(0, n_dom - 1)
+        return remote(wfull.at[:, most], wfull.at[:, most], wp_s, wp_r, (mate, z))
+
+    def b_copy(o):
+        return remote(bfull.at[z], bfull.at[z], b_s, b_r, (d, lax.rem(z + o, n_col)))
+
+    def b_copies():
+        some = bfull.at[pl.ds(0, n_col - 1)]
+        return remote(some, some, b_s, b_r, (d, lax.rem(z + 1, n_col)))
+
     for copy in first_tables:
         copy.wait()
     gather_early(peer_of(0))
     pl.semaphore_wait(barrier, n_dom - 1 + n_col - 1)
     halo_send(0, peer_of(0)).start()
+    w_load().wait()
+    for o in range(1, n_col):
+        w_copy(o).start()
+        b_copy(o).start()
 
     @pl.loop(1, n_chips - 1)
     def _(i):
@@ -265,31 +290,6 @@
     def _(i):
         halo_send(1, peer_of(i)).start()
 
-    def w_copy(o):
-        return remote(wfull.at[z, d], wfull.at[z, d], w_s, w_r, (d, lax.rem(z + o, n_col)))
-
-    def w_copies():
-        some = pl.ds(0, n_col - 1)
-        return remote(wfull.at[some, d], wfull.at[some, d], w_s, w_r, (d, lax.rem(z + 1, n_col)))
-
-    def w_pass(o):
-        return remote(wfull.at[:, d], wfull.at[:, d], wp_s, wp_r, (lax.rem(d + o, n_dom), z))
-
-    def w_passes():
-        most = pl.ds(0, n_dom - 1)
-        return remote(wfull.at[:, most], wfull.at[:, most], wp_s, wp_r, (mate, z))
-
-    def b_copy(o):
-        return remote(bfull.at[z], bfull.at[z], b_s, b_r, (d, lax.rem(z + o, n_col)))
-
-    def b_copies():
-        some = bfull.at[pl.ds(0, n_col - 1)]
-        return remote(some, some, b_s, b_r, (d, lax.rem(z + 1, n_col)))
-
-    w_load().wait()
-    for o in range(1, n_col):
-        w_copy(o).start()
-        b_copy(o).start()
 
     @pl.loop(n_chips - 1, n_dom - 1)
     def _(i):
@@ -297,7 +297,7 @@
         halo_send(0, peer_of(i)).start()
         halo_send(1, peer_of(i)).start()
 
-    @pl.when(core == 1)
+    @pl.when(core == 0)
     def _():
         widen_late()
         gather_late()
@@ -411,7 +411,7 @@
     def _(s):
         own_step(s)
 
-    @pl.when(core == 0)
+    @pl.when(core == 1)
     def _():
         widen_late()
         gather_late()

time: 200 us -> 200 us (level); the launches traced: 200 us -> 196 us
  Pallas kernels: 199 us -> 196 us
    pallas_call x1, Pallas kernels: 197 us -> 194 us  [on_device(): pl.pallas_call(functools.partial(kernel, n_dom, n_col, rows * n_dom), out...]
where the time goes in v6:
time: 200 us; the launch traced here: 196 us
  Pallas kernels  196 us (98%)
    pallas_call x1, Pallas kernels, on_device(): pl.pallas_call(functools.partial(kernel, n_dom, n_col, rows * n_dom), out...  194 us

profile of v6, /device:TPU:1, one launch (start us, length us, event | category | flops | bytes accessed | tf_op | source)
XLA Modules:
  0.0 196.4 jit_solution(17296361138747531369)
XLA Ops:
  0.6 193.7 %shard_map.122 = (bf16[8192,256]{1,0:T(8,128)(2,1)S(1)}, f32[2,256]{1,0:T(2,128)S(1)}) custom-call(bf16[64,128,256]{2,1,0:T(8,128)(2,1)} %bitcast.12, bf16[1024,256]{1,0:T(8,128)(2,1)} %weight_hbm.1, bf16[256]{0:T(256)(128)(2,1)} %bias_ref.1, s32[4,64]{1,0:T(4,128)} %bitcast.14, s32[1,64]{1,0:T(1,128)} %lcnt_hbm.1, bf16[64,4,128,128]{3,2,1,0:T(8,128)(2,1)} %bitcast.10, ...), custom_call_target="tpu_custom_call" | custom-call | tf_op jit(solution)/shard_map/pallas_call | solution.py:591
  194.4 2.0 %shard_map.123 = (bf16[8192,256]{1,0:T(8,128)(2,1)}, f32[2,256]{1,0:T(2,128)}) custom-call(bf16[8192,256]{1,0:T(8,128)(2,1)S(1)} %get-tuple-element.4.rows_ref, f32[2,256]{1,0:T(2,128)S(1)} %get-tuple-element.5.stat_ref), custom_call_target="tpu_custom_call" | custom-call | tf_op jit(solution)/shard_map/pallas_call | solution.py:670
